TPU v7x, 256 devices: a whole 4x4x8 slice. The times are simulated.
256 devices in a mesh: occ: 4 (over z_lo), vir: 64 (over y, x, z_hi, core).
Axes of the slice: x: 4, y: 4, z: 8 (z_hi: 2, z_lo: 4; z = z_hi * 4 + z_lo), core: 2. Of those that a mesh axis runs over, the one named last changes fastest.
Arguments:
- amplitudes: bfloat16 [352, 32768], P('occ', 'vir'), may hold values from -6 to 6
- integrals: bfloat16 [32768, 32768], P('vir', 'occ'), may hold values from -0.25 to 0.25
- labels: int32 [256], replicated, may hold values from 0 to 7
- slot_tile: int32 [256], replicated, may hold values from 0 to 255, each once
Outputs:
- residual: float32 [352, 32768], P(None, ('occ', 'vir'))
Inputs may be any that keep to these rules, and one draw needn't show every extreme that they name: `slot_tile`: each tile appears in exactly one slot.
All inputs are finite; a program needn't handle non-finite values.
Results may differ from a plain program's by a relative error of at most 0.0003.
Values may be sent and summed in bfloat16 or wider, within the bound.
A program may use at most 128 MiB of HBM per device.

v0:
```python
import jax
import jax.numpy as jnp
from jax import lax
from jax.sharding import Mesh
from jax.sharding import PartitionSpec as P

TILE = 128
VIR = ("vir_0", "vir_1", "vir_2", "vir_3")
OCC_VIR = ("occ", "vir_0", "vir_1", "vir_2", "vir_3")


def joined_along(parts, dim):
    shape = list(parts.shape[1:])
    shape[dim] *= parts.shape[0]
    return jnp.moveaxis(parts, 0, dim).reshape(shape)


def from_everyone(value, axis):
    peers = lax.axis_size(axis)
    return lax.all_to_all(
        jnp.broadcast_to(value[None], (peers, *value.shape)), axis, 0, 0, tiled=True
    )


def collect(value, axis, dim):
    return joined_along(from_everyone(value, axis), dim)


def in_blocks(value, dim, peers):
    shape = value.shape
    parts = value.reshape(*shape[:dim], peers, shape[dim] // peers, *shape[dim + 1 :])
    return jnp.moveaxis(parts, dim, 0)


def summed_rows(value, chips, core, dim):
    sizes = (lax.axis_size(chips), lax.axis_size(core))
    parts = in_blocks(value, dim, sizes[0] * sizes[1])
    inside = parts.shape[1:]
    parts = parts.reshape(*sizes, *inside).swapaxes(0, 1).reshape(-1, *inside)
    parts = lax.psum_scatter(parts, core, scatter_dimension=0, tiled=True)
    return lax.psum_scatter(parts, chips, scatter_dimension=0, tiled=True)[0]


def shards(amplitudes, integrals, labels, slot_tile):
    vir_index = lax.axis_index(VIR)
    occ_index = lax.axis_index("occ")
    local_slots = integrals.shape[0] // TILE
    ab_tiles = integrals.shape[1] // TILE
    my_slots = lax.dynamic_slice_in_dim(slot_tile, vir_index * local_slots, local_slots)
    slot_label = labels[my_slots]
    ab_label = lax.dynamic_slice_in_dim(labels, occ_index * ab_tiles, ab_tiles)
    keep = (slot_label[:, None] == ab_label[None, :]).astype(jnp.bfloat16)
    keep_full = jnp.repeat(jnp.repeat(keep, TILE, axis=0), TILE, axis=1)
    masked = integrals * keep_full
    gathered = collect(amplitudes, "occ", 0)
    summed = summed_rows(
        lax.dot_general(
            masked, gathered, (((0,), (1,)), ((), ())), preferred_element_type=jnp.float32
        ),
        ("vir_0", "vir_1", "vir_2"),
        "vir_3",
        0,
    )
    return jnp.transpose(summed)


def solution(mesh):
    split = Mesh(
        mesh.devices.reshape(mesh.shape["occ"], 4, 4, 2, 2),
        ("occ", "vir_0", "vir_1", "vir_2", "vir_3"),
    )
    placed = (P("occ", VIR), P(VIR, "occ"), P(), P())
    return jax.shard_map(
        shards, mesh=split, in_specs=placed, out_specs=P(None, OCC_VIR), check_vma=False
    )
```

profile of v0, /device:TPU:32, one launch (start us, length us, event | category | flops | bytes accessed | tf_op | source)
XLA Modules:
  0.0 391.3 jit_solution(11747468549251092840)
XLA Ops:
  6.5 1.7 broadcast_in_dim.20
  8.2 6.0 %all-to-all-start = ((bf16[4,88,512]{2,1,0:T(8,128)(2,1)}), bf16[4,88,512]{2,1,0:T(8,128)(2,1)S(1)}, u32[]{:S(2)}, u32[]{:S(2)}) async-start(bf16[4,88,512]{2,1,0:T(8,128)(2,1)} %broadcast_in_dim.20), calls=%async_computation | async-start | bytes 720896 | tf_op jit(solution)/shard_map/all_to_all | solution.py:20
  14.2 0.0 reduce-scatter.3.cloned.1.call-start
  14.2 0.8 compare_select_fusion
  15.0 0.8 dynamic_slice.7
  15.7 1.3 gather_fusion
  17.1 0.0 copy-start
  17.1 0.1 compare_convert_fusion
  17.2 6.3 %broadcast_in_dim.19 = bf16[512,64,128]{2,1,0:T(8,128)(2,1)S(1)} broadcast(bf16[512,64]{1,0:T(8,128)(2,1)S(1)} %bitcast.26), dimensions={0,1} | broadcast | bytes 8454144 | tf_op jit(solution)/shard_map/broadcast_in_dim | solution.py:53
  23.4 0.0 copy-done
  23.4 6.4 %fusion = bf16[8192,512]{0,1:T(8,128)(2,1)} fusion(bf16[512,8192]{1,0:T(8,128)(2,1)S(1)} %copy-done, bf16[64,8,64,128]{3,2,1,0:T(8,128)(2,1)S(1)} %bitcast.24), kind=kLoop, calls=%fused_computation.2 | loop fusion | flops 4194304 | bytes 25165824 | tf_op jit(solution)/shard_map/dot_general | solution.py:57
  29.9 12.0 %copy.9 = bf16[8192,512]{1,0:T(8,128)(2,1)} copy(bf16[8192,512]{0,1:T(8,128)(2,1)} %fusion) | data formatting | bytes 16777216 | tf_op jit(solution)/shard_map/dot_general | solution.py:57
  41.9 0.0 all-to-all-done
  41.9 11.7 %convolution_bitcast_fusion = f32[2,32,128,352]{2,3,0,1:T(8,128)} fusion(bf16[32,2,128,512]{3,2,1,0:T(8,128)(2,1)} %bitcast.22, bf16[352,512,1,1]{1,0,3,2:T(8,128)(2,1)S(1)} %bitcast.25), kind=kOutput, calls=%fused_computation.3 | convolution fusion | flops 2952790016 | bytes 20283392 | tf_op jit(solution)/shard_map/dot_general | solution.py:57
  53.5 9.4 %copy.7 = f32[2,32,128,352]{2,3,1,0:T(8,128)} copy(f32[2,32,128,352]{2,3,0,1:T(8,128)} %convolution_bitcast_fusion) | data formatting | bytes 23068672 | tf_op jit(solution)/shard_map/transpose | solution.py:39
  62.9 0.0 reduce-scatter.3.cloned.1.call-update
  62.9 0.0 reduce-scatter.5.cloned.1.call-start
  63.0 25.0 %reduce-scatter.3.cloned.1.call-done = f32[32,128,352]{1,2,0:T(8,128)} async-done(((f32[64,128,352]{1,2,0:T(8,128)}), f32[32,128,352]{1,2,0:T(8,128)}) %reduce-scatter.3.cloned.1.call-update) | async-done | bytes 5767184 | tf_op jit(solution)/shard_map/reduce_scatter | solution.py:40
  87.9 0.0 reduce-scatter.5.cloned.1.call-update
  87.9 296.6 %reduce-scatter.5.cloned.1.call-done = f32[1,128,352]{1,2,0:T(8,128)} async-done(((f32[32,128,352]{1,2,0:T(8,128)}), f32[1,128,352]{1,2,0:T(8,128)}) %reduce-scatter.5.cloned.1.call-update) | async-done | bytes 180240 | tf_op jit(solution)/shard_map/reduce_scatter | solution.py:41
  (2 shorter events, 0.0 us)
Async XLA Ops:
  8.2 33.6 %all-to-all-start = ((bf16[4,88,512]{2,1,0:T(8,128)(2,1)}), bf16[4,88,512]{2,1,0:T(8,128)(2,1)S(1)}, u32[]{:S(2)}, u32[]{:S(2)}) async-start(bf16[4,88,512]{2,1,0:T(8,128)(2,1)} %broadcast_in_dim.20), calls=%async_computation | async-start | bytes 720896 | tf_op jit(solution)/shard_map/all_to_all | solution.py:20
  14.2 73.7 %reduce-scatter.3.cloned.1.call-start = ((), (), s32[]{:S(2)}) async-start(), calls=%async_computation.3 | async-start | bytes 17301504 | tf_op jit(solution)/shard_map/reduce_scatter | solution.py:40
  17.1 6.4 %copy-start = (bf16[512,8192]{1,0:T(8,128)(2,1)S(1)}, bf16[512,8192]{1,0:T(8,128)(2,1)}, u32[]{:S(2)}) copy-start(bf16[512,8192]{1,0:T(8,128)(2,1)} %param.5) | copy-start | bytes 25165828
  62.9 321.6 %reduce-scatter.5.cloned.1.call-start = ((), (), s32[]{:S(2)}) async-start(), calls=%async_computation.4 | async-start | bytes 5947392 | tf_op jit(solution)/shard_map/reduce_scatter | solution.py:41
Sparse Core Ops, SparseCore 0:
  63.0 24.8 reduce-scatter.2
  90.5 293.9 reduce-scatter.4
where the time goes:
time: 392 us; the launch traced here: 391 us
  waiting for transfers between devices  322 us (82%)
  local copies, waits for them, and re-layouts  31.4 us (8%)
  between operations  13.4 us (3%)
  matrix products  11.7 us (3%)
  other arithmetic  7.28 us (2%)
  starting transfers between devices  6.04 us (2%)
    reduce_scatter x1, waiting for transfers between devices, summed_rows(): return lax.psum_scatter(parts, chips, scatter_dimension=0, tiled=True)[0]  297 us
    reduce_scatter x1, waiting for transfers between devices, summed_rows(): parts = lax.psum_scatter(parts, core, scatter_dimension=0, tiled=True)  25 us
    dot_general x1, local copies, waits for them, and re-layouts, shards(): lax.dot_general(masked, gathered, (((0,), (1,)), ((), ())), preferred_ele...  12 us
    dot_general x1, matrix products, shards(): lax.dot_general(masked, gathered, (((0,), (1,)), ((), ())), preferred_ele...  11.7 us
    transpose x1, local copies, waits for them, and re-layouts, summed_rows(): parts = parts.reshape(*sizes, *inside).swapaxes(0, 1).reshape(-1, *inside)  9.36 us
  transfers between devices with their start and end apart: 3, of which 2 were waited for; matrix products, arithmetic and copies ran while one was open for 7% of the time, Pallas kernels for 0%

commit v1 on v0

v1 whole, which is shorter than its diff:
```python
import functools

import jax
import jax.numpy as jnp
from jax import lax
from jax.experimental import pallas as pl
from jax.experimental.pallas import tpu as pltpu
from jax.sharding import Mesh
from jax.sharding import PartitionSpec as P

TILE = 128
VIR = ("vir_0", "vir_1", "vir_2", "vir_3")
OCC_VIR = ("occ", "vir_0", "vir_1", "vir_2", "vir_3")
MESH = pl.DeviceIdType.MESH
CHUNKS = 4
LOG_STEP = 350.0
TOP = 32700.0


def coded(value):
    rows = value.shape[0]
    parts = value.reshape(rows // 8, 8, TILE)
    largest = jnp.maximum(jnp.max(jnp.abs(parts), axis=0), 1e-30)
    level = jnp.ceil(jnp.log(largest) * LOG_STEP)
    scaled = parts * (jnp.exp(level * (-1.0 / LOG_STEP)) * TOP)[None]
    scaled = jnp.round(scaled).reshape(rows, TILE)
    pad = [level] if rows % 16 else [level, level]
    return jnp.concatenate([scaled, *pad], axis=0).astype(jnp.int32).astype(jnp.int16)


def decoded(message, rows):
    value = message.astype(jnp.int32).astype(jnp.float32)
    scale = jnp.exp(value[rows : rows + 8] * (1.0 / LOG_STEP)) * (1.0 / TOP)
    parts = value[:rows].reshape(rows // 8, 8, TILE) * scale[None]
    return parts.reshape(rows, TILE)


def kernel(
    rows,
    amp_ref, int_ref, labels_ref, slot_ref, out_ref,
    amp, own, other, acc, plane, tower, s1, r1, s2, r2, s3, r3,
    own_sem, swap_send, swap_recv, amp_sem, mate_send, mate_recv, occ_send, occ_recv,
    s1_sem, r1_sem, s2_sem, r2_sem, s3_sem, r3_sem,
):
    occ = lax.axis_index("occ")
    y, x, zh, core = (lax.axis_index(name) for name in VIR)
    vir = ((y * 4 + x) * 2 + zh) * 2 + core
    mate = 1 - core
    blocks = [occ, occ + 1 - 2 * lax.rem(occ, 2), lax.rem(occ + 2, 4), 3 - occ]
    place = {"vir_0": y, "vir_1": x}
    up = {axis: lax.rem(at + 1, 4) for axis, at in place.items()}
    down = {axis: lax.rem(at + 3, 4) for axis, at in place.items()}
    far = {axis: lax.rem(at + 2, 4) for axis, at in place.items()}

    def copy_to(src, dst, send, recv, device):
        return pltpu.make_async_remote_copy(
            src_ref=src, dst_ref=dst, send_sem=send, recv_sem=recv,
            device_id=device, device_id_type=MESH,
        )

    def columns(pair, half, parity):
        tile = (pair * 2 + half) * 2 + parity
        return int_ref.at[:, pl.ds(pl.multiple_of(tile * TILE, TILE), TILE)]

    for pair in range(16):
        for half in range(2):
            pltpu.make_async_copy(
                columns(pair, half, core),
                own.at[pair, :, pl.ds(half * TILE, TILE)],
                own_sem.at[pair // 4],
            ).start()
    own_amp = pltpu.make_async_copy(amp_ref, amp.at[occ, core], amp_sem)
    own_amp.start()

    barrier = pltpu.get_barrier_semaphore()
    partners = [{"vir_3": mate}, {"vir_2": 1 - zh}]
    for axis in place:
        partners += [{axis: up[axis]}, {axis: down[axis]}]
    partners += [{"occ": block} for block in blocks[1:]]
    for partner in partners:
        pl.semaphore_signal(barrier, inc=1, device_id=partner, device_id_type=MESH)
    pl.semaphore_wait(barrier, len(partners))

    sent = []

    def send(*args):
        copy = copy_to(*args)
        copy.start()
        sent.append(copy)

    send(amp_ref, amp.at[occ, core], mate_send.at[0], mate_recv.at[occ], {"vir_3": mate})
    for step in range(1, CHUNKS):
        send(
            amp_ref, amp.at[occ, core], occ_send.at[step], occ_recv.at[occ],
            {"occ": blocks[step]},
        )
    for pair in range(16):
        for half in range(2):
            copy_to(
                columns(pair, half, mate),
                other.at[pair, :, pl.ds(half * TILE, TILE)],
                swap_send.at[pair // 4], swap_recv.at[pair // 4], {"vir_3": mate},
            ).start()

    def group_wait(buffer, group, sem):
        part = buffer.at[pl.ds(group * 4, 4)]
        pltpu.make_async_copy(part, part, sem.at[group]).wait()

    def forward(step):
        block = blocks[step]
        here = amp.at[block, core]
        copy_to(here, here, occ_send.at[step], occ_recv.at[block], {"occ": block}).wait_recv()
        send(here, here, mate_send.at[step], mate_recv.at[block], {"vir_3": mate})

    lane = lax.broadcasted_iota(jnp.int32, (1, 2 * TILE), 1)
    own_first = vir * 4
    other_first = (vir + 1 - 2 * core) * 4

    def keep(first, pair, slot):
        label = labels_ref[slot_ref[first + slot]]
        tile = occ * 64 + pair * 4 + core
        low = jnp.where(label == labels_ref[tile], 1.0, 0.0)
        high = jnp.where(label == labels_ref[tile + 2], 1.0, 0.0)
        return jnp.where(lane < TILE, low, high).astype(jnp.bfloat16)

    def compute(step):
        block = blocks[step]
        if step == 0:
            own_amp.wait()
        there = amp.at[block, mate]
        copy_to(there, there, mate_send.at[step], mate_recv.at[block], {"vir_3": mate}).wait_recv()

        for group in range(4):
            if step == 0:
                group_wait(own, group, own_sem)
                group_wait(other, group, swap_recv)

            def one(pair, _):
                pair = pair + group * 4
                if step == 0:
                    for buffer, first in ((own, own_first), (other, other_first)):
                        for slot in range(4):
                            at = pl.ds(slot * TILE, TILE)
                            buffer[pair, at, :] = buffer[pair, at, :] * keep(first, pair, slot)
                acc[step, pair] = jnp.dot(
                    amp[block, core], own[pair], preferred_element_type=jnp.float32
                ) + jnp.dot(
                    amp[block, mate], other[pair], preferred_element_type=jnp.float32
                )
                return 0

            lax.fori_loop(0, 4, one, 0, unroll=True)

    FIRST = ("vir_1", "vir_0")
    SECOND = ("vir_0", "vir_1")

    def two_tiles(step, colour, target, part):
        found = []
        for other_at in (2 * part, 2 * part + 1):
            pair = other_at * 4 + target if colour == 0 else target * 4 + other_at
            found.append(acc[step, pair, :, pl.ds(colour * TILE, TILE)])
        return jnp.concatenate(found, axis=0)

    def send1(step, colour, way, kind, value):
        axis = FIRST[colour]
        at = (step, colour, way, kind)
        s1[at] = coded(value)
        send(
            s1.at[at], r1.at[at], s1_sem.at[at], r1_sem.at[at],
            {axis: (up, down)[way][axis]},
        )

    def take1(step, colour, way, kind):
        at = (step, colour, way, kind)
        axis = FIRST[colour]
        copy_to(
            s1.at[at], r1.at[at], s1_sem.at[at], r1_sem.at[at], {axis: up[axis]}
        ).wait_recv()
        return decoded(r1[at], 2 * rows)

    def first_send(step):
        for colour in range(2):
            axis = FIRST[colour]
            for way in range(2):
                send1(step, colour, way, 0, two_tiles(step, colour, far[axis], way))
        for colour in range(2):
            axis = FIRST[colour]
            for way in range(2):
                near = (up, down)[way][axis]
                send1(step, colour, way, 1, two_tiles(step, colour, near, 1 - way))

    def first_relay(step):
        for colour in range(2):
            axis = FIRST[colour]
            for way in range(2):
                near = (up, down)[way][axis]
                send1(
                    step, colour, way, 2,
                    take1(step, colour, way, 0) + two_tiles(step, colour, near, way),
                )

    def send2(step, colour, way, kind, value):
        axis = SECOND[colour]
        at = (step, colour, kind)
        s2[at] = coded(value)
        send(
            s2.at[at], r2.at[at], s2_sem.at[at], r2_sem.at[at],
            {axis: (up, down)[way][axis]},
        )

    def take2(step, colour, kind):
        at = (step, colour, kind)
        axis = SECOND[colour]
        copy_to(
            s2.at[at], r2.at[at], s2_sem.at[at], r2_sem.at[at], {axis: up[axis]}
        ).wait_recv()
        return decoded(r2[at], rows)

    def first_end(step):
        for colour in range(2):
            axis = FIRST[colour]
            for part in range(2):
                total = (
                    two_tiles(step, colour, place[axis], part)
                    + take1(step, colour, 1 - part, 1)
                    + take1(step, colour, part, 2)
                )
                plane[step, colour, 2 * part] = total[:rows]
                plane[step, colour, 2 * part + 1] = total[rows:]
            way = step % 2
            axis = SECOND[colour]
            send2(step, colour, way, 0, plane[step, colour, far[axis]])
            back = (down, up)[way][axis]
            send2(step, colour, 1 - way, 1, plane[step, colour, back])

    def second_relay(step):
        way = step % 2
        for colour in range(2):
            near = (up, down)[way][SECOND[colour]]
            send2(
                step, colour, way, 2,
                take2(step, colour, 0) + plane[step, colour, near],
            )

    def second_end(step):
        for colour in range(2):
            here = place[SECOND[colour]]
            tower[step, colour] = (
                plane[step, colour, here] + take2(step, colour, 1) + take2(step, colour, 2)
            )
        s3[step] = coded(tower[step, 1 - zh])
        send(s3.at[step], r3.at[step], s3_sem.at[step], r3_sem.at[step], {"vir_2": 1 - zh})

    def finish(step):
        copy_to(
            s3.at[step], r3.at[step], s3_sem.at[step], r3_sem.at[step], {"vir_2": 1 - zh}
        ).wait_recv()
        at = pl.ds(pl.multiple_of(blocks[step] * rows, 8), rows)
        out_ref[at, :] = tower[step, zh] + decoded(r3[step], rows)

    stages = (compute, first_send, first_relay, first_end, second_relay, second_end, finish)
    for tick in range(CHUNKS + 5):
        for step in range(CHUNKS - 1, -1, -1):
            age = tick - step
            if age == 0:
                if step + 1 < CHUNKS:
                    forward(step + 1)
                compute(step)
                first_send(step)
            elif 0 < age < 6:
                stages[age + 1](step)

    for copy in sent:
        copy.wait_send()
    for group in range(4):
        group_wait(own, group, swap_send)


def shards(amplitudes, integrals, labels, slot_tile):
    rows = amplitudes.shape[0]
    depth = integrals.shape[0]
    vmem = pltpu.VMEM
    dma = pltpu.SemaphoreType.DMA
    first = (CHUNKS, 2, 2, 3)
    second = (CHUNKS, 2, 3)
    return pl.pallas_call(
        functools.partial(kernel, rows),
        out_shape=jax.ShapeDtypeStruct((CHUNKS * rows, TILE), jnp.float32),
        in_specs=[
            pl.BlockSpec(memory_space=pl.ANY),
            pl.BlockSpec(memory_space=pl.ANY),
            pl.BlockSpec(memory_space=pltpu.SMEM),
            pl.BlockSpec(memory_space=pltpu.SMEM),
        ],
        out_specs=pl.BlockSpec(memory_space=vmem),
        scratch_shapes=[
            vmem((CHUNKS, 2, rows, depth), jnp.bfloat16),
            vmem((16, depth, 2 * TILE), jnp.bfloat16),
            vmem((16, depth, 2 * TILE), jnp.bfloat16),
            vmem((CHUNKS, 16, rows, 2 * TILE), jnp.float32),
            vmem((CHUNKS, 2, 4, rows, TILE), jnp.float32),
            vmem((CHUNKS, 2, rows, TILE), jnp.float32),
            vmem((*first, 2 * rows + 16, TILE), jnp.int16),
            vmem((*first, 2 * rows + 16, TILE), jnp.int16),
            vmem((*second, rows + 8, TILE), jnp.int16),
            vmem((*second, rows + 8, TILE), jnp.int16),
            vmem((CHUNKS, rows + 8, TILE), jnp.int16),
            vmem((CHUNKS, rows + 8, TILE), jnp.int16),
            dma((4,)), dma((4,)), dma((4,)), dma,
            dma((CHUNKS,)), dma((CHUNKS,)), dma((CHUNKS,)), dma((CHUNKS,)),
            dma(first), dma(first), dma(second), dma(second), dma((CHUNKS,)), dma((CHUNKS,)),
        ],
        compiler_params=pltpu.CompilerParams(
            collective_id=0, has_side_effects=True, vmem_limit_bytes=48 * 1024 * 1024
        ),
        name="ladder",
    )(amplitudes, integrals, labels, slot_tile)


def solution(mesh):
    split = Mesh(
        mesh.devices.reshape(mesh.shape["occ"], 4, 4, 2, 2),
        ("occ", "vir_0", "vir_1", "vir_2", "vir_3"),
    )
    placed = (P("occ", VIR), P(VIR, "occ"), P(), P())
    return jax.shard_map(
        shards, mesh=split, in_specs=placed, out_specs=P(None, OCC_VIR), check_vma=False
    )
```

time: 392 us -> 51.7 us (0.13)
  the two profiles are of different devices: /device:TPU:32 before, /device:TPU:6 now
where the time goes in v1:
time: 51.7 us; the launch traced here: 51.6 us
  Pallas kernels  48.6 us (94%)
  local copies, waits for them, and re-layouts  2.92 us (6%)
    pallas_call x1, Pallas kernels, shards(): pl.pallas_call(functools.partial(kernel, rows), out_shape=jax.ShapeDtypeS...  48.6 us
    unnamed x7, local copies, waits for them, and re-layouts  2.92 us

profile of v1, /device:TPU:6, one launch (start us, length us, event | category | flops | bytes accessed | tf_op | source)
XLA Modules:
  0.0 51.6 jit_solution(14478636342658900536)
XLA Ops:
  0.0 0.0 copy-start
  0.0 0.9 %copy-done = bf16[88,512]{1,0:T(8,128)(2,1)S(1)} copy-done((bf16[88,512]{1,0:T(8,128)(2,1)S(1)}, bf16[88,512]{1,0:T(8,128)(2,1)}, u32[]{:S(2)}) %copy-start) | copy-done | bytes 90136
  0.9 0.0 copy-start.1
  0.9 0.7 %copy-done.1 = s32[256]{0:T(256)S(1)} copy-done((s32[256]{0:T(256)S(1)}, s32[256]{0:T(256)}, u32[]{:S(2)}) %copy-start.1) | copy-done | bytes 1048
  1.6 0.0 copy-start.2
  1.6 0.7 %copy-done.2 = s32[256]{0:T(256)S(1)} copy-done((s32[256]{0:T(256)S(1)}, s32[256]{0:T(256)}, u32[]{:S(2)}) %copy-start.2) | copy-done | bytes 1048
  2.2 48.6 %ladder.1 = f32[352,128]{1,0:T(8,128)S(1)} custom-call(bf16[88,512]{1,0:T(8,128)(2,1)S(1)} %copy-done, bf16[512,8192]{1,0:T(8,128)(2,1)} %int_ref.1, s32[256]{0:T(256)S(1)} %copy-done.1, s32[256]{0:T(256)S(1)} %copy-done.2), custom_call_target="tpu_custom_call" | custom-call | tf_op jit(solution)/shard_map/ladder/pallas_call | solution.py:286
  50.9 0.7 %copy.6 = f32[352,128]{1,0:T(8,128)} copy(f32[352,128]{1,0:T(8,128)S(1)} %ladder.1) | data formatting | bytes 360448
Async XLA Ops:
  0.0 0.9 %copy-start = (bf16[88,512]{1,0:T(8,128)(2,1)S(1)}, bf16[88,512]{1,0:T(8,128)(2,1)}, u32[]{:S(2)}) copy-start(bf16[88,512]{1,0:T(8,128)(2,1)} %amp_ref.1) | copy-start | bytes 270340
  0.9 0.7 %copy-start.1 = (s32[256]{0:T(256)S(1)}, s32[256]{0:T(256)}, u32[]{:S(2)}) copy-start(s32[256]{0:T(256)} %labels_ref.1) | copy-start | bytes 3076
  1.6 0.7 %copy-start.2 = (s32[256]{0:T(256)S(1)}, s32[256]{0:T(256)}, u32[]{:S(2)}) copy-start(s32[256]{0:T(256)} %slot_ref.1) | copy-start | bytes 3076

commit v2 on v0

v2 whole, which is shorter than its diff:
```python
import functools

import jax
import jax.numpy as jnp
from jax import lax
from jax.experimental import pallas as pl
from jax.experimental.pallas import tpu as pltpu
from jax.sharding import Mesh
from jax.sharding import PartitionSpec as P

TILE = 128
VIR = ("vir_0", "vir_1", "vir_2", "vir_3")
OCC_VIR = ("occ", "vir_0", "vir_1", "vir_2", "vir_3")
MESH = pl.DeviceIdType.MESH
CHUNKS = 4
LOG_STEP = 350.0
TOP = 32700.0


def coded(value):
    rows = value.shape[0]
    parts = value.reshape(rows // 8, 8, TILE)
    largest = jnp.maximum(jnp.max(jnp.abs(parts), axis=0), 1e-30)
    level = jnp.ceil(jnp.log(largest) * LOG_STEP)
    scaled = parts * (jnp.exp(level * (-1.0 / LOG_STEP)) * TOP)[None]
    scaled = jnp.round(scaled).reshape(rows, TILE)
    pad = [level] if rows % 16 else [level, level]
    return jnp.concatenate([scaled, *pad], axis=0).astype(jnp.int32).astype(jnp.int16)


def decoded(message, rows):
    value = message.astype(jnp.int32).astype(jnp.float32)
    scale = jnp.exp(value[rows : rows + 8] * (1.0 / LOG_STEP)) * (1.0 / TOP)
    parts = value[:rows].reshape(rows // 8, 8, TILE) * scale[None]
    return parts.reshape(rows, TILE)


def kernel(
    rows, parts, order, direct,
    amp_ref, int_ref, labels_ref, slot_ref, out_ref,
    labels, slots, amp, integ, acc, macc, plane, tower, s1, r1, s2, r2, s3, r3,
    small_sem, int_sem, ready_sem, occ_send, occ_recv, mate_send, mate_recv,
    s1_sem, r1_sem, s2_sem, r2_sem, s3_sem, r3_sem,
):
    occ = lax.axis_index("occ")
    y, x, zh, core = (lax.axis_index(name) for name in VIR)
    vir = ((y * 4 + x) * 2 + zh) * 2 + core
    mate = 1 - core
    inner = jnp.logical_and(occ > 0, occ < 3)
    two_on, opposite = lax.rem(occ + 2, 4), 3 - occ
    blocks = [
        occ, occ + 1 - 2 * lax.rem(occ, 2),
        jnp.where(inner, opposite, two_on), jnp.where(inner, two_on, opposite),
    ]
    place = {"vir_0": y, "vir_1": x}
    up = {axis: lax.rem(at + 1, 4) for axis, at in place.items()}
    down = {axis: lax.rem(at + 3, 4) for axis, at in place.items()}
    far = {axis: lax.rem(at + 2, 4) for axis, at in place.items()}
    FIRST = ("vir_1", "vir_0")
    SECOND = ("vir_0", "vir_1")

    def copy_to(src, dst, send, recv, device):
        return pltpu.make_async_remote_copy(
            src_ref=src, dst_ref=dst, send_sem=send, recv_sem=recv,
            device_id=device, device_id_type=MESH,
        )

    def pair_of(colour, dest, j):
        return j * 4 + dest if colour == 0 else dest * 4 + j

    def wait_for(part, sem):
        pltpu.make_async_copy(part, part, sem).wait()

    small = [
        pltpu.make_async_copy(labels_ref, labels, small_sem.at[0]),
        pltpu.make_async_copy(slot_ref, slots, small_sem.at[1]),
        pltpu.make_async_copy(amp_ref, amp.at[occ], small_sem.at[2]),
    ]
    for copy in small:
        copy.start()
    def fetch(turn, _):
        steps = jnp.where(turn < 2, 2 - turn, 3 * (3 - turn))
        for colour in range(2):
            dest = lax.rem(place[FIRST[colour]] + steps, 4)
            for j in range(4):
                first = (pair_of(colour, dest, j) * 2 + colour) * 2 * TILE
                pltpu.make_async_copy(
                    int_ref.at[:, pl.ds(pl.multiple_of(first, 2 * TILE), 2 * TILE)],
                    integ.at[colour, dest, j],
                    int_sem.at[colour, dest],
                ).start()
        return 0

    lax.fori_loop(0, 4, fetch, 0)

    barrier = pltpu.get_barrier_semaphore()
    partners = [{"vir_3": mate}]
    for axis in place:
        partners += [{axis: up[axis]}, {axis: down[axis]}, {axis: far[axis]}]
    partners += [{"occ": block} for block in blocks[1:]]
    for partner in partners:
        pl.semaphore_signal(barrier, inc=1, device_id=partner, device_id_type=MESH)

    @pl.when(zh == 0)
    def _():
        pl.semaphore_signal(barrier, inc=1, device_id={"vir_2": 1 - zh}, device_id_type=MESH)

    def send(*args):
        copy_to(*args).start()

    def keep(colour, dest, j, slot):
        label = labels[slots[vir * 4 + slot]]
        tile = occ * 64 + (pair_of(colour, dest, j) * 2 + colour) * 2
        lane = lax.broadcasted_iota(jnp.int32, (1, 2 * TILE), 1)
        low = jnp.where(label == labels[tile], 1.0, 0.0)
        high = jnp.where(label == labels[tile + 1], 1.0, 0.0)
        return jnp.where(lane < TILE, low, high).astype(jnp.bfloat16)

    def multiply(step, colour, dest):
        if step == 0:
            wait_for(integ.at[colour, dest], int_sem.at[colour, dest])
        for j in range(4):
            if step == 0:
                for slot in range(4):
                    at = pl.ds(slot * TILE, TILE)
                    integ[colour, dest, j, at, :] = (
                        integ[colour, dest, j, at, :] * keep(colour, dest, j, slot)
                    )
            found = jnp.dot(
                amp[blocks[step]], integ[colour, dest, j], preferred_element_type=jnp.float32
            )
            for parity in range(2):
                acc[step, parity, colour, dest, j] = found[:, parity * TILE : (parity + 1) * TILE]

    groups = {id(far): (0, 1), id(up): (2, 2), id(down): (2, 2), id(place): (3, 3)}

    def units(step, where):
        for colour in range(2):
            multiply(step, colour, where[FIRST[colour]])

    def hand_over(step, where):
        for colour in range(2):
            dest = where[FIRST[colour]]
            send(
                acc.at[step, mate, colour, dest], macc.at[step, colour, dest],
                mate_send.at[step], mate_recv.at[step, groups[id(where)][colour]],
                {"vir_3": mate},
            )

    taken = set()

    def take_over(chunk, group):
        step = parts[chunk][0]
        if (step, group) not in taken:
            taken.add((step, group))
            part = (
                macc.at[step, 0, 0], macc.at[step, 0, 0],
                macc.at[step, 0], macc.at[step, 0, pl.ds(0, 2)],
            )[group]
            wait_for(part, mate_recv.at[step, group])

    def to_peer(step):
        send(
            amp.at[occ], amp.at[occ], occ_send, occ_recv.at[occ], {"occ": blocks[step]}
        )

    def product(step):
        wait_for(amp.at[blocks[step]], occ_recv.at[blocks[step]])
        for where in (far, up, down, place):
            units(step, where)
            hand_over(step, where)

    def two_tiles(chunk, colour, target, part):
        step, start, count = parts[chunk]
        at = (colour, target, pl.ds(2 * part, 2), pl.ds(start, count))
        return (acc[(step, core, *at)] + macc[(step, *at)]).reshape(2 * count, TILE)

    def message(buffer, at, count):
        return buffer.at[(*at, pl.ds(0, count + 16 - count % 16))]

    def send1(chunk, colour, way, kind, value):
        axis = FIRST[colour]
        at = (chunk, colour, way, kind)
        out = message(s1, at, value.shape[0])
        out[...] = coded(value)
        send(
            out, message(r1, at, value.shape[0]),
            s1_sem.at[chunk], r1_sem.at[chunk, colour, min(kind, 1)],
            {axis: (up, down)[way][axis]},
        )

    def sizes(chunk):
        count = parts[chunk][2]
        return pl.ds(0, 2 * count + 16), pl.ds(0, count + 16 - count % 16)

    def take1(chunk, colour, way, kind):
        count = 2 * parts[chunk][2]
        return decoded(message(r1, (chunk, colour, way, kind), count)[...], count)

    def first_far(chunk):
        for colour in range(2):
            take_over(chunk, colour)
            for way in range(2):
                value = two_tiles(chunk, colour, far[FIRST[colour]], way)
                send1(chunk, colour, way, 0, value)

    def first_near(chunk):
        take_over(chunk, 2)
        for way in range(2):
            for colour in range(2):
                near = (up, down)[way]
                value = two_tiles(chunk, colour, near[FIRST[colour]], 1 - way)
                send1(chunk, colour, way, 1, value)

    def first_send(chunk):
        first_far(chunk)
        first_near(chunk)

    def first_relay(chunk):
        for colour in range(2):
            wait_for(r1.at[chunk, colour, :, 0, sizes(chunk)[0]], r1_sem.at[chunk, colour, 0])
            for way in range(2):
                near = (up, down)[way][FIRST[colour]]
                value = two_tiles(chunk, colour, near, way)
                send1(chunk, colour, way, 2, take1(chunk, colour, way, 0) + value)

    def send2(chunk, colour, kind, value, target):
        at = (chunk, colour, kind)
        out = message(s2, at, value.shape[0])
        out[...] = coded(value)
        send(
            out, message(r2, at, value.shape[0]),
            s2_sem.at[chunk], r2_sem.at[chunk, min(kind, 1)],
            {SECOND[colour]: target[SECOND[colour]]},
        )

    def take2(chunk, colour, kind):
        count = parts[chunk][2]
        return decoded(message(r2, (chunk, colour, kind), count)[...], count)

    def arrive2(chunk, group):
        kinds = pl.ds(0, 1) if group == 0 else pl.ds(1, 2)
        wait_for(r2.at[chunk, :, kinds, sizes(chunk)[1]], r2_sem.at[chunk, group])

    def ways(chunk):
        return (up, down) if chunk % 2 == 0 else (down, up)

    def first_end(chunk):
        onward, back = ways(chunk)
        step, start, count = parts[chunk]
        at = pl.ds(start, count)
        for colour in range(2):
            axis = FIRST[colour]
            take_over(chunk, 3)
            wait_for(
                r1.at[chunk, colour, :, pl.ds(1, 2), sizes(chunk)[0]],
                r1_sem.at[chunk, colour, 1],
            )
            for part in range(2):
                total = (
                    two_tiles(chunk, colour, place[axis], part)
                    + take1(chunk, colour, 1 - part, 1)
                    + take1(chunk, colour, part, 2)
                )
                plane[step, colour, 2 * part, at] = total[:count]
                plane[step, colour, 2 * part + 1, at] = total[count:]
            axis = SECOND[colour]
            to_far = far if chunk in direct else onward
            send2(chunk, colour, 0, plane[step, colour, far[axis], at], to_far)
            send2(chunk, colour, 1, plane[step, colour, back[axis], at], back)
            if chunk in direct:
                send2(chunk, colour, 2, plane[step, colour, onward[axis], at], onward)

    def second_relay(chunk):
        if chunk in direct:
            return
        onward, _ = ways(chunk)
        step, start, count = parts[chunk]
        arrive2(chunk, 0)
        for colour in range(2):
            value = plane[step, colour, onward[SECOND[colour]], pl.ds(start, count)]
            send2(chunk, colour, 2, take2(chunk, colour, 0) + value, onward)

    def second_end(chunk):
        step, start, count = parts[chunk]
        at = pl.ds(start, count)
        if chunk in direct:
            arrive2(chunk, 0)
        arrive2(chunk, 1)
        for colour in range(2):
            total = plane[step, colour, place[SECOND[colour]], at]
            for kind in range(0 if chunk in direct else 1, 3):
                total = total + take2(chunk, colour, kind)
            tower[step, colour, at] = total
        out = message(s3, (chunk,), count)
        out[...] = coded(tower[step, 1 - zh, at])
        if chunk == 0:

            @pl.when(zh == 0)
            def _():
                pl.semaphore_wait(ready_sem, 1)

        send(
            out, message(r3, (chunk,), count), s3_sem.at[chunk], r3_sem.at[chunk],
            {"vir_2": 1 - zh},
        )

    def finish(chunk):
        step, start, count = parts[chunk]
        here = message(r3, (chunk,), count)
        wait_for(here, r3_sem.at[chunk])
        at = pl.ds(pl.multiple_of(blocks[step] * rows + start, 8), count)
        out_ref[at, :] = tower[step, zh, pl.ds(start, count)] + decoded(here[...], count)

    for copy in small:
        copy.wait()
    units(0, far)

    pl.semaphore_wait(barrier, len(partners) + zh)

    to_peer(1)

    @pl.when(zh == 1)
    def _():
        pl.semaphore_signal(ready_sem, inc=1, device_id={"vir_2": 1 - zh}, device_id_type=MESH)

    @pl.when(inner)
    def _():
        to_peer(2)
        to_peer(3)

    hand_over(0, far)
    units(0, up)
    hand_over(0, up)
    units(0, down)
    hand_over(0, down)
    first_far(0)
    units(0, place)
    hand_over(0, place)
    first_near(0)

    @pl.when(jnp.logical_not(inner))
    def _():
        to_peer(2)
        to_peer(3)


    stages = {
        "P": product, "S": first_send, "R": first_relay, "F": first_end,
        "G": second_relay, "H": second_end, "Z": finish,
    }
    for row in order:
        for kind, number in zip(row[::2], row[1::2]):
            stages[kind](int(number))

    wait_for(amp.at[pl.ds(0, CHUNKS - 1)], occ_send)
    for step in range(CHUNKS):
        wait_for(acc.at[step, mate], mate_send.at[step])
    for chunk in range(len(parts)):
        wait_for(s1.at[chunk, :, :, :, sizes(chunk)[0]], s1_sem.at[chunk])
        wait_for(s2.at[chunk, :, :, sizes(chunk)[1]], s2_sem.at[chunk])
        wait_for(s3.at[chunk, sizes(chunk)[1]], s3_sem.at[chunk])


PARTS = ((0, 0, 88), (1, 0, 88), (2, 0, 88), (3, 0, 48), (3, 48, 40))
DIRECT = (3, 4)
ORDER = (
    "P1R0S1P2F0R1S2P3G0F1R2S3S4H0G1F2R3R4H1",
    "G2F3F4H2H3H4Z0Z1Z2Z3Z4",
)


def shards(amplitudes, integrals, labels, slot_tile):
    rows = amplitudes.shape[0]
    depth = integrals.shape[0]
    vmem = pltpu.VMEM
    dma = pltpu.SemaphoreType.DMA
    third = (len(PARTS),)
    first = (*third, 2, 2, 3)
    second = (*third, 2, 3)
    return pl.pallas_call(
        functools.partial(kernel, rows, PARTS, ORDER, DIRECT),
        out_shape=vmem((CHUNKS * rows, TILE), jnp.float32),
        in_specs=[pl.BlockSpec(memory_space=pltpu.HBM)] * 4,
        out_specs=pl.BlockSpec(memory_space=vmem),
        scratch_shapes=[
            pltpu.SMEM(labels.shape, jnp.int32),
            pltpu.SMEM(slot_tile.shape, jnp.int32),
            vmem((CHUNKS, rows, depth), jnp.bfloat16),
            vmem((2, 4, 4, depth, 2 * TILE), jnp.bfloat16),
            vmem((CHUNKS, 2, 2, 4, 4, rows, TILE), jnp.float32),
            vmem((CHUNKS, 2, 4, 4, rows, TILE), jnp.float32),
            vmem((CHUNKS, 2, 4, rows, TILE), jnp.float32),
            vmem((CHUNKS, 2, rows, TILE), jnp.float32),
            vmem((*first, 2 * rows + 16, TILE), jnp.int16),
            vmem((*first, 2 * rows + 16, TILE), jnp.int16),
            vmem((*second, rows + 8, TILE), jnp.int16),
            vmem((*second, rows + 8, TILE), jnp.int16),
            vmem((*third, rows + 8, TILE), jnp.int16),
            vmem((*third, rows + 8, TILE), jnp.int16),
            dma((3,)), dma((2, 4)), pltpu.SemaphoreType.REGULAR, dma, dma((CHUNKS,)), dma((CHUNKS,)), dma((CHUNKS, 4)),
            dma(third), dma((*third, 2, 2)), dma(third), dma((*third, 2)), dma(third), dma(third),
        ],
        compiler_params=pltpu.CompilerParams(
            collective_id=0, has_side_effects=True, vmem_limit_bytes=60 * 1024 * 1024
        ),
        name="ladder",
    )(amplitudes, integrals, labels, slot_tile)


def solution(mesh):
    split = Mesh(
        mesh.devices.reshape(mesh.shape["occ"], 4, 4, 2, 2),
        ("occ", "vir_0", "vir_1", "vir_2", "vir_3"),
    )
    placed = (P("occ", VIR), P(VIR, "occ"), P(), P())
    return jax.shard_map(
        shards, mesh=split, in_specs=placed, out_specs=P(None, OCC_VIR), check_vma=False
    )
```

time: 392 us -> 42.6 us (0.11)
  the two profiles are of different devices: /device:TPU:32 before, /device:TPU:6 now
where the time goes in v2:
time: 42.6 us; the launch traced here: 42.1 us
  Pallas kernels  41.5 us (97%)
  local copies, waits for them, and re-layouts  0.67 us (2%)
    pallas_call x1, Pallas kernels, shards(): pl.pallas_call(functools.partial(kernel, rows, PARTS, ORDER, DIRECT), out...  41.5 us

profile of v2, /device:TPU:6, one launch (start us, length us, event | category | flops | bytes accessed | tf_op | source)
XLA Modules:
  0.0 42.1 jit_solution(4078816516133869822)
XLA Ops:
  0.0 41.5 %ladder.1 = f32[352,128]{1,0:T(8,128)S(1)} custom-call(bf16[88,512]{1,0:T(8,128)(2,1)} %amp_ref.1, bf16[512,8192]{1,0:T(8,128)(2,1)} %int_ref.1, s32[256]{0:T(256)} %labels_ref.1, s32[256]{0:T(256)} %slot_ref.1), custom_call_target="tpu_custom_call" | custom-call | tf_op jit(solution)/shard_map/ladder/pallas_call | solution.py:381
  41.5 0.7 %copy.6 = f32[352,128]{1,0:T(8,128)} copy(f32[352,128]{1,0:T(8,128)S(1)} %ladder.1) | data formatting | bytes 360448

commit v3 on v2

--- a/solution.py
+++ b/solution.py
@@ -24,8 +24,7 @@
     level = jnp.ceil(jnp.log(largest) * LOG_STEP)
     scaled = parts * (jnp.exp(level * (-1.0 / LOG_STEP)) * TOP)[None]
     scaled = jnp.round(scaled).reshape(rows, TILE)
-    pad = [level] if rows % 16 else [level, level]
-    return jnp.concatenate([scaled, *pad], axis=0).astype(jnp.int32).astype(jnp.int16)
+    return jnp.concatenate([scaled, level], axis=0).astype(jnp.int32).astype(jnp.int16)
 
 
 def decoded(message, rows):
@@ -176,7 +175,7 @@
         return (acc[(step, core, *at)] + macc[(step, *at)]).reshape(2 * count, TILE)
 
     def message(buffer, at, count):
-        return buffer.at[(*at, pl.ds(0, count + 16 - count % 16))]
+        return buffer.at[(*at, pl.ds(0, count + 8))]
 
     def send1(chunk, colour, way, kind, value):
         axis = FIRST[colour]
@@ -191,38 +190,35 @@
 
     def sizes(chunk):
         count = parts[chunk][2]
-        return pl.ds(0, 2 * count + 16), pl.ds(0, count + 16 - count % 16)
+        return pl.ds(0, 2 * count + 8), pl.ds(0, count + 8)
 
     def take1(chunk, colour, way, kind):
         count = 2 * parts[chunk][2]
         return decoded(message(r1, (chunk, colour, way, kind), count)[...], count)
 
-    def first_far(chunk):
-        for colour in range(2):
-            take_over(chunk, colour)
-            for way in range(2):
-                value = two_tiles(chunk, colour, far[FIRST[colour]], way)
-                send1(chunk, colour, way, 0, value)
-
-    def first_near(chunk):
+    def first_far(chunk, colour):
+        take_over(chunk, colour)
+        for way in range(2):
+            value = two_tiles(chunk, colour, far[FIRST[colour]], way)
+            send1(chunk, colour, way, 0, value)
+
+    def first_near(chunk, colour):
         take_over(chunk, 2)
         for way in range(2):
-            for colour in range(2):
-                near = (up, down)[way]
-                value = two_tiles(chunk, colour, near[FIRST[colour]], 1 - way)
-                send1(chunk, colour, way, 1, value)
-
-    def first_send(chunk):
-        first_far(chunk)
-        first_near(chunk)
-
-    def first_relay(chunk):
-        for colour in range(2):
-            wait_for(r1.at[chunk, colour, :, 0, sizes(chunk)[0]], r1_sem.at[chunk, colour, 0])
-            for way in range(2):
-                near = (up, down)[way][FIRST[colour]]
-                value = two_tiles(chunk, colour, near, way)
-                send1(chunk, colour, way, 2, take1(chunk, colour, way, 0) + value)
+            near = (up, down)[way]
+            value = two_tiles(chunk, colour, near[FIRST[colour]], 1 - way)
+            send1(chunk, colour, way, 1, value)
+
+    def first_send(chunk, colour):
+        first_far(chunk, colour)
+        first_near(chunk, colour)
+
+    def first_relay(chunk, colour):
+        wait_for(r1.at[chunk, colour, :, 0, sizes(chunk)[0]], r1_sem.at[chunk, colour, 0])
+        for way in range(2):
+            near = (up, down)[way][FIRST[colour]]
+            value = two_tiles(chunk, colour, near, way)
+            send1(chunk, colour, way, 2, take1(chunk, colour, way, 0) + value)
 
     def send2(chunk, colour, kind, value, target):
         at = (chunk, colour, kind)
@@ -230,7 +226,7 @@
         out[...] = coded(value)
         send(
             out, message(r2, at, value.shape[0]),
-            s2_sem.at[chunk], r2_sem.at[chunk, min(kind, 1)],
+            s2_sem.at[chunk], r2_sem.at[chunk, colour, min(kind, 1)],
             {SECOND[colour]: target[SECOND[colour]]},
         )
 
@@ -238,72 +234,67 @@
         count = parts[chunk][2]
         return decoded(message(r2, (chunk, colour, kind), count)[...], count)
 
-    def arrive2(chunk, group):
+    def arrive2(chunk, colour, group):
         kinds = pl.ds(0, 1) if group == 0 else pl.ds(1, 2)
-        wait_for(r2.at[chunk, :, kinds, sizes(chunk)[1]], r2_sem.at[chunk, group])
+        wait_for(r2.at[chunk, colour, kinds, sizes(chunk)[1]], r2_sem.at[chunk, colour, group])
 
     def ways(chunk):
         return (up, down) if chunk % 2 == 0 else (down, up)
 
-    def first_end(chunk):
+    def first_end(chunk, colour):
         onward, back = ways(chunk)
         step, start, count = parts[chunk]
         at = pl.ds(start, count)
-        for colour in range(2):
-            axis = FIRST[colour]
-            take_over(chunk, 3)
-            wait_for(
-                r1.at[chunk, colour, :, pl.ds(1, 2), sizes(chunk)[0]],
-                r1_sem.at[chunk, colour, 1],
+        axis = FIRST[colour]
+        take_over(chunk, 3)
+        wait_for(
+            r1.at[chunk, colour, :, pl.ds(1, 2), sizes(chunk)[0]], r1_sem.at[chunk, colour, 1]
+        )
+        for part in range(2):
+            total = (
+                two_tiles(chunk, colour, place[axis], part)
+                + take1(chunk, colour, 1 - part, 1)
+                + take1(chunk, colour, part, 2)
             )
-            for part in range(2):
-                total = (
-                    two_tiles(chunk, colour, place[axis], part)
-                    + take1(chunk, colour, 1 - part, 1)
-                    + take1(chunk, colour, part, 2)
-                )
-                plane[step, colour, 2 * part, at] = total[:count]
-                plane[step, colour, 2 * part + 1, at] = total[count:]
-            axis = SECOND[colour]
-            to_far = far if chunk in direct else onward
-            send2(chunk, colour, 0, plane[step, colour, far[axis], at], to_far)
-            send2(chunk, colour, 1, plane[step, colour, back[axis], at], back)
-            if chunk in direct:
-                send2(chunk, colour, 2, plane[step, colour, onward[axis], at], onward)
-
-    def second_relay(chunk):
+            plane[step, colour, 2 * part, at] = total[:count]
+            plane[step, colour, 2 * part + 1, at] = total[count:]
+        axis = SECOND[colour]
+        to_far = far if chunk in direct else onward
+        send2(chunk, colour, 0, plane[step, colour, far[axis], at], to_far)
+        send2(chunk, colour, 1, plane[step, colour, back[axis], at], back)
+        if chunk in direct:
+            send2(chunk, colour, 2, plane[step, colour, onward[axis], at], onward)
+
+    def second_relay(chunk, colour):
         if chunk in direct:
             return
         onward, _ = ways(chunk)
         step, start, count = parts[chunk]
-        arrive2(chunk, 0)
-        for colour in range(2):
-            value = plane[step, colour, onward[SECOND[colour]], pl.ds(start, count)]
-            send2(chunk, colour, 2, take2(chunk, colour, 0) + value, onward)
-
-    def second_end(chunk):
+        arrive2(chunk, colour, 0)
+        value = plane[step, colour, onward[SECOND[colour]], pl.ds(start, count)]
+        send2(chunk, colour, 2, take2(chunk, colour, 0) + value, onward)
+
+    def second_end(chunk, colour):
         step, start, count = parts[chunk]
         at = pl.ds(start, count)
         if chunk in direct:
-            arrive2(chunk, 0)
-        arrive2(chunk, 1)
-        for colour in range(2):
-            total = plane[step, colour, place[SECOND[colour]], at]
-            for kind in range(0 if chunk in direct else 1, 3):
-                total = total + take2(chunk, colour, kind)
-            tower[step, colour, at] = total
-        out = message(s3, (chunk,), count)
-        out[...] = coded(tower[step, 1 - zh, at])
-        if chunk == 0:
-
-            @pl.when(zh == 0)
-            def _():
+            arrive2(chunk, colour, 0)
+        arrive2(chunk, colour, 1)
+        total = plane[step, colour, place[SECOND[colour]], at]
+        for kind in range(0 if chunk in direct else 1, 3):
+            total = total + take2(chunk, colour, kind)
+        tower[step, colour, at] = total
+
+        @pl.when(zh == 1 - colour)
+        def _():
+            out = message(s3, (chunk,), count)
+            out[...] = coded(total)
+            if chunk == 0 and colour == 1:
                 pl.semaphore_wait(ready_sem, 1)
-
-        send(
-            out, message(r3, (chunk,), count), s3_sem.at[chunk], r3_sem.at[chunk],
-            {"vir_2": 1 - zh},
-        )
+            send(
+                out, message(r3, (chunk,), count), s3_sem.at[chunk], r3_sem.at[chunk],
+                {"vir_2": 1 - zh},
+            )
 
     def finish(chunk):
         step, start, count = parts[chunk]
@@ -334,10 +325,12 @@
     hand_over(0, up)
     units(0, down)
     hand_over(0, down)
-    first_far(0)
+    for colour in range(2):
+        first_far(0, colour)
     units(0, place)
     hand_over(0, place)
-    first_near(0)
+    for colour in range(2):
+        first_near(0, colour)
 
     @pl.when(jnp.logical_not(inner))
     def _():
@@ -346,12 +339,16 @@
 
 
     stages = {
-        "P": product, "S": first_send, "R": first_relay, "F": first_end,
-        "G": second_relay, "H": second_end, "Z": finish,
+        "s": first_send, "r": first_relay, "f": first_end, "g": second_relay, "h": second_end
     }
     for row in order:
         for kind, number in zip(row[::2], row[1::2]):
-            stages[kind](int(number))
+            if kind == "P":
+                product(int(number))
+            elif kind == "Z":
+                finish(int(number))
+            else:
+                stages[kind.lower()](int(number), int(kind.isupper()))
 
     wait_for(amp.at[pl.ds(0, CHUNKS - 1)], occ_send)
     for step in range(CHUNKS):
@@ -365,8 +362,9 @@
 PARTS = ((0, 0, 88), (1, 0, 88), (2, 0, 88), (3, 0, 48), (3, 48, 40))
 DIRECT = (3, 4)
 ORDER = (
-    "P1R0S1P2F0R1S2P3G0F1R2S3S4H0G1F2R3R4H1",
-    "G2F3F4H2H3H4Z0Z1Z2Z3Z4",
+    "P1r0R0s1S1P2f0r1s2R1S2P3g0f1r2s3s4F0R2S3S4",
+    "h0g1f2r3r4G0F1R3R4h1g2f3f4H0G1F2h2F3h3F4h4",
+    "H1G2H2H3H4Z0Z1Z2Z3Z4",
 )
 
 
@@ -392,14 +390,14 @@
             vmem((CHUNKS, 2, 4, 4, rows, TILE), jnp.float32),
             vmem((CHUNKS, 2, 4, rows, TILE), jnp.float32),
             vmem((CHUNKS, 2, rows, TILE), jnp.float32),
-            vmem((*first, 2 * rows + 16, TILE), jnp.int16),
-            vmem((*first, 2 * rows + 16, TILE), jnp.int16),
+            vmem((*first, 2 * rows + 8, TILE), jnp.int16),
+            vmem((*first, 2 * rows + 8, TILE), jnp.int16),
             vmem((*second, rows + 8, TILE), jnp.int16),
             vmem((*second, rows + 8, TILE), jnp.int16),
             vmem((*third, rows + 8, TILE), jnp.int16),
             vmem((*third, rows + 8, TILE), jnp.int16),
             dma((3,)), dma((2, 4)), pltpu.SemaphoreType.REGULAR, dma, dma((CHUNKS,)), dma((CHUNKS,)), dma((CHUNKS, 4)),
-            dma(third), dma((*third, 2, 2)), dma(third), dma((*third, 2)), dma(third), dma(third),
+            dma(third), dma((*third, 2, 2)), dma(third), dma((*third, 2, 2)), dma(third), dma(third),
         ],
         compiler_params=pltpu.CompilerParams(
             collective_id=0, has_side_effects=True, vmem_limit_bytes=60 * 1024 * 1024

time: 42.6 us -> 41.4 us (0.972)
  Pallas kernels: 41.5 us -> 40.6 us
    pallas_call x1, Pallas kernels: 41.5 us -> 40.6 us  [shards(): pl.pallas_call(functools.partial(kernel, rows, PARTS, ORDER, DIRECT), out...]
where the time goes in v3:
time: 41.4 us; the launch traced here: 41.3 us
  Pallas kernels  40.6 us (98%)
  local copies, waits for them, and re-layouts  0.67 us (2%)
    pallas_call x1, Pallas kernels, shards(): pl.pallas_call(functools.partial(kernel, rows, PARTS, ORDER, DIRECT), out...  40.6 us

profile of v3, /device:TPU:6, one launch (start us, length us, event | category | flops | bytes accessed | tf_op | source)
XLA Modules:
  0.0 41.3 jit_solution(3462853885014339607)
XLA Ops:
  0.0 40.6 %ladder.1 = f32[352,128]{1,0:T(8,128)S(1)} custom-call(bf16[88,512]{1,0:T(8,128)(2,1)} %amp_ref.1, bf16[512,8192]{1,0:T(8,128)(2,1)} %int_ref.1, s32[256]{0:T(256)} %labels_ref.1, s32[256]{0:T(256)} %slot_ref.1), custom_call_target="tpu_custom_call" | custom-call | tf_op jit(solution)/shard_map/ladder/pallas_call | solution.py:379
  40.6 0.7 %copy.6 = f32[352,128]{1,0:T(8,128)} copy(f32[352,128]{1,0:T(8,128)S(1)} %ladder.1) | data formatting | bytes 360448
